TPU v7x, 512 devices: a whole 4x4x16 slice. The times are simulated.
512 devices in a mesh: lon: 32 (over z, core), lat: 4 (over y), lev: 4 (over x).
Axes of the slice: x: 4, y: 4, z: 16, core: 2. Of those that a mesh axis runs over, the one named last changes fastest.
Arguments:
- fields: float32 [3, 8, 960, 512], P(None, 'lev', 'lon', 'lat'), may hold values from -6 to 6
- spectral_coeffs: float32 [3, 8], P(None, 'lev'), may hold values from 0.3 to 3
- mlp_in: bfloat16 [384, 24], replicated, may hold values from -1.25 to 1.25
- mlp_mid: bfloat16 [2, 384, 384], replicated, may hold values from -0.3125 to 0.3125
- mlp_out: bfloat16 [24, 384], replicated, may hold values from -0.3125 to 0.3125
Outputs:
- updated: float32 [3, 8, 960, 512], P(None, 'lev', 'lon', 'lat')
All inputs are finite; a program needn't handle non-finite values.
Results may differ from a plain program's by a relative error of at most 0.0012.
Values may be sent and summed in bfloat16 or wider, within the bound.
A program may use at most 64 MiB of HBM per device.

v0:
```python
import functools

import jax
import jax.numpy as jnp
import numpy as np
from jax import lax
from jax.experimental import pallas as pl
from jax.experimental.pallas import tpu as pltpu
from jax.sharding import PartitionSpec as P

WAVES = 320
KMAX = 320
SUBSTEPS = 2
NLON = 960
NLAT = 512
LEVELS = 8
UNITS = 384
GROUP = 64
F32 = jnp.float32
BF16 = jnp.bfloat16


def split_host(table):
    high = table.astype(np.float32).astype(BF16)
    low = (table - high.astype(np.float64)).astype(np.float32).astype(BF16)
    return np.stack([high, low])


@functools.lru_cache(None)
def host_tables():
    q = np.repeat(np.arange(10), GROUP)
    o = np.tile(np.arange(GROUP), 10)
    wave = 2 * (5 * (o // 2) + q % 5) + o % 2
    lane = np.arange(1024)
    lon = 30 * (lane // 32) + lane % 32
    phase = (wave[:, None] * lon[None, :]) % NLON * (2.0 * np.pi / NLON)
    zonal = np.where(q[:, None] < 5, np.cos(phase), -np.sin(phase)) * (lane % 32 < 30)[None, :]
    pos = np.arange(NLAT)
    lat = 8 * (pos % 64) + pos // 64
    deg = np.arange(KMAX)
    odd = 2 * lat + 1
    even = np.cos((deg[:, None] * odd[None, :]) % (4 * NLAT) * (np.pi / (2 * NLAT)))
    sine = np.sin(((deg[:, None] + 1) * odd[None, :]) % (4 * NLAT) * (np.pi / (2 * NLAT)))
    fwd = np.stack([split_host(even), split_host(sine)])
    inv = np.stack([split_host(even.T), split_host(sine.T)])
    perm = np.zeros((10, 24, 256), np.float32)
    for f in range(3):
        for i8 in range(8):
            for c in range(10):
                perm[c, f * 8 + i8, i8 * 32 + f * 10 + c] = 1.0
    gather = np.concatenate([perm, perm], axis=1).reshape(480, 256).astype(BF16)
    scatter = perm.reshape(240, 256).astype(BF16)
    return split_host(zonal), fwd, inv, gather, scatter


def split(value):
    high = value.astype(BF16)
    return high, (value - high.astype(F32)).astype(BF16)


def mm(a, b):
    return lax.dot_general(a, b, (((1,), (0,)), ((), ())), preferred_element_type=F32)


def mm_nt(a, b):
    return lax.dot_general(a, b, (((1,), (1,)), ((), ())), preferred_element_type=F32)


def silu(v):
    return 0.5 * v * (1.0 + jnp.tanh(0.5 * v))


def kernel(
    coef_ref, fields_hbm, zonal_hbm, fwd_hbm, inv_hbm, gather_hbm, scatter_hbm, w_in_hbm, w_mid_hbm, w_out_hbm,
    out_ref,
    fields, zonal, fwd, inv, gather, scatter, w_in, w_mid, w_out,
    stage, at, ra, state, vb, ub, mult, mb, rm, cr, fb, ob,
    load_sems, send_sems, recv_sems,
):
    zc = lax.axis_index("lon")
    y = lax.axis_index("lat")
    x = lax.axis_index("lev")
    z, c = lax.div(zc, 2), lax.rem(zc, 2)
    p, zb = lax.div(z, 2), lax.rem(z, 2)
    mine = x * 4 + zb * 2 + c
    me = y * 16 + mine
    own_x, own_b = lax.rem(p, 4), lax.div(p, 4)

    loads = []

    def load(n, src, dst):
        copy = pltpu.make_async_copy(src, dst, load_sems.at[n])
        copy.start()
        loads.append(copy)

    load(0, fields_hbm, fields)
    load(1, zonal_hbm, zonal)
    load(2, fwd_hbm.at[c], fwd)
    load(3, inv_hbm.at[c], inv)
    load(4, gather_hbm, gather)
    load(5, scatter_hbm, scatter)
    load(6, w_in_hbm, w_in)
    load(7, w_mid_hbm, w_mid)
    load(8, w_out_hbm, w_out)

    def group_device(g):
        return {"lon": 4 * p + lax.rem(g, 4), "lat": lax.div(g, 16), "lev": lax.div(lax.rem(g, 16), 4)}

    def first_target(t):
        b, k = lax.div(t, 16), lax.rem(t, 16)
        return {"lon": 4 * (x + 4 * b) + lax.rem(k, 4), "lat": y, "lev": lax.div(k, 4)}

    own_first = x == own_x
    self_t = own_b * 16 + mine

    barrier = pltpu.get_barrier_semaphore()

    def greet_first(j, carry):
        d = lax.rem(zc + j, 32)

        @pl.when(jnp.logical_or(d != zc, jnp.logical_not(own_first)))
        def _():
            pl.semaphore_signal(barrier, inc=1, device_id={"lon": d, "lat": y, "lev": own_x})
        return carry

    def greet_group(j, carry):
        pl.semaphore_signal(barrier, inc=1, device_id=group_device(lax.rem(me + j, GROUP)))
        return carry

    def greet_planes(j, carry):
        pl.semaphore_signal(barrier, inc=1, device_id={"lon": 2 * lax.rem(z + j, 16) + c, "lat": y, "lev": x})
        return carry

    lax.fori_loop(0, 32, greet_first, 0)
    lax.fori_loop(1, GROUP, greet_group, 0)
    lax.fori_loop(1, 16, greet_planes, 0)

    loads[0].wait()
    for b in range(2):
        for f in range(3):
            stage[32 * f : 32 * f + 30, :] = fields[f, b]
            stage[32 * f + 30 : 32 * f + 32, :] = jnp.zeros((2, 128), F32)
        for n in range(3):
            stage[96 + n : 97 + n, :] = jnp.full((1, 128), coef_ref[n, b], F32)
        stage[99:128, :] = jnp.zeros((29, 128), F32)
        at[128 * b : 128 * b + 128, :] = stage[...].T

    pl.semaphore_wait(barrier, 31 + jnp.where(own_first, 0, 1) + (GROUP - 1) + 15)

    def send_first(j, carry):
        t = lax.rem(self_t + j, 32)

        @pl.when(jnp.logical_or(j > 0, jnp.logical_not(own_first)))
        def _():
            pltpu.make_async_remote_copy(
                at.at[pl.ds(pl.multiple_of(8 * t, 8), 8), :],
                ra.at[pl.ds(pl.multiple_of(8 * zc, 8), 8), :],
                send_sems.at[0], recv_sems.at[0], device_id=first_target(t),
            ).start()
        return carry

    lax.fori_loop(0, 32, send_first, 0)

    @pl.when(own_first)
    def _():
        ra[pl.ds(pl.multiple_of(8 * zc, 8), 8), :] = at[pl.ds(pl.multiple_of(8 * self_t, 8), 8), :]

    def drain(ref, sem):
        pltpu.make_async_copy(ref, ref, sem).wait()

    for n in range(1, 9):
        loads[n].wait()

    @pl.when(own_first)
    def _():
        drain(ra.at[pl.ds(0, 248), :], recv_sems.at[0])

    @pl.when(jnp.logical_not(own_first))
    def _():
        drain(ra, recv_sems.at[0])

    lane = lax.broadcasted_iota(jnp.int32, (8, 128), 1)
    for v in range(8):
        tiles = [ra[8 * (4 * v + n) : 8 * (4 * v + n) + 8, :] for n in range(4)]
        for f in range(3):
            value = pltpu.roll(tiles[0], (-32 * f) % 128, 1)
            for n in range(1, 4):
                value = jnp.where(lane >= 32 * n, pltpu.roll(tiles[n], (32 * (n - f)) % 128, 1), value)
            state[8 * f : 8 * f + 8, 128 * v : 128 * v + 128] = value

    coefs = ra[0:1, :]

    def operator_tables():
        nu, ga, gb = coefs[:, 96:97], coefs[:, 97:98], coefs[:, 98:99]
        deg = lax.broadcasted_iota(jnp.int32, (KMAX, 32), 0)
        col = lax.broadcasted_iota(jnp.int32, (KMAX, 32), 1)
        field = jnp.where(col >= 20, 2, jnp.where(col >= 10, 1, 0))
        place = col - 10 * field
        turn = jnp.where(place >= 5, place - 5, place)
        wave = 2 * (5 * lax.div(me, 2) + turn) + c
        freq = (deg + c).astype(F32)
        wavef = wave.astype(F32)
        qv = (wavef * wavef + freq * freq) / (KMAX * KMAX)
        scale = jnp.where(wave == 0, 1.0, 2.0) * (2.0 / NLAT / NLON)
        damp = nu * qv * qv
        couple = ga * gb * qv
        den = 1.0 + jnp.where(field == 0, damp, couple)
        own = -jnp.where(field == 0, damp, couple)
        other = jnp.where(field == 0, 0.0, jnp.where(field == 1, ga * qv, -gb))
        valid = col < 30
        factor = jnp.where(valid, scale / den, 0.0)
        mult[0] = own * factor
        mult[1] = other * factor

    for step in range(SUBSTEPS):
        b_in, c_in = 2 * step, 2 * step + 1

        high, low = split(state[...])
        both = jnp.concatenate([high.astype(F32), low.astype(F32)], axis=0).astype(BF16)
        first = jnp.concatenate([high.astype(F32), jnp.zeros((24, 1024), F32)], axis=0).astype(BF16)
        value = mm_nt(zonal[0], both) + mm_nt(zonal[1], first)
        w_high, w_low = split(value)
        packed = jnp.zeros((GROUP, 256), F32)
        for q in range(10):
            rows = slice(GROUP * q, GROUP * q + GROUP)
            place = gather[48 * q : 48 * q + 48, :]
            packed = packed + mm(w_high[rows], place) + mm(w_low[rows], place)

        def exchange(n, value):
            vb[n, pl.ds(0, GROUP, stride=2), :] = value[:, :128]
            vb[n, pl.ds(1, GROUP, stride=2), :] = value[:, 128:]

            def send(j, carry):
                g = lax.rem(me + j, GROUP)
                pltpu.make_async_remote_copy(
                    vb.at[n, pl.ds(2 * g, 2), :], ub.at[n, pl.ds(2 * me, 2), :],
                    send_sems.at[1 + n], recv_sems.at[1 + n], device_id=group_device(g),
                ).start()
                return carry

            lax.fori_loop(1, GROUP, send, 0, unroll=True)
            ub[n, pl.ds(2 * me, 2), :] = vb[n, pl.ds(2 * me, 2), :]

        def received(n):
            drain(ub.at[n, pl.ds(0, 2 * GROUP - 2), :], recv_sems.at[1 + n])
            return jnp.concatenate(
                [ub[n, pl.ds(0, GROUP, stride=2), :], ub[n, pl.ds(1, GROUP, stride=2), :]], axis=1
            )

        exchange(b_in, packed)
        if step == 0:
            operator_tables()
        value = received(b_in)

        value = jnp.concatenate([value[:, 32 * n : 32 * n + 32] for n in range(8)], axis=0)
        high, low = split(value)
        spectra = mm(fwd[0], high) + mm(fwd[0], low) + mm(fwd[1], high)
        col = lax.broadcasted_iota(jnp.int32, (KMAX, 32), 1)
        up = jnp.concatenate([spectra[:, 10:], spectra[:, :10]], axis=1)
        down = jnp.concatenate([spectra[:, 22:], spectra[:, :22]], axis=1)
        change = spectra * mult[0] + jnp.where(col < 20, up, down) * mult[1]
        high, low = split(change)
        value = mm(inv[0], high) + mm(inv[0], low) + mm(inv[1], high)
        value = jnp.concatenate([value[64 * n : 64 * n + 64] for n in range(8)], axis=1)

        exchange(c_in, value)
        value = received(c_in)

        high, low = split(value)
        y_high = mm_nt(scatter[...], high)
        y_low = mm_nt(scatter[...], low)
        y_high = jnp.concatenate([y_high[24 * q : 24 * q + 24] for q in range(10)], axis=1)
        y_low = jnp.concatenate([y_low[24 * q : 24 * q + 24] for q in range(10)], axis=1)
        both = jnp.concatenate([y_high, y_low], axis=0).astype(BF16)
        value = mm(both, zonal[0])
        new = state[...] + value[:24] + value[24:] + mm(y_high.astype(BF16), zonal[1])
        state[0:16, :] = new[0:16]
        state[16:24, :] = new[16:24] + 0.25 * new[0:8] * new[8:16]

    half = lane < 64
    for t in range(16):
        v = t // 2
        s = [state[8 * f : 8 * f + 8, 128 * v : 128 * v + 128] for f in range(3)]
        if t % 2 == 0:
            mb[16 * t : 16 * t + 8, :] = jnp.where(half, s[0], pltpu.roll(s[1], 64, 1))
            mb[16 * t + 8 : 16 * t + 16, :] = s[2]
        else:
            mb[16 * t : 16 * t + 8, :] = jnp.where(half, pltpu.roll(s[0], 64, 1), s[1])
            mb[16 * t + 8 : 16 * t + 16, :] = pltpu.roll(s[2], 64, 1)
    slot = zb * 8 + 2 * own_x + own_b

    def send_planes(j, carry):
        t = lax.rem(z + j, 16)
        pltpu.make_async_remote_copy(
            mb.at[pl.ds(pl.multiple_of(16 * t, 16), 16), :], rm.at[pl.ds(pl.multiple_of(16 * slot, 16), 16), :],
            send_sems.at[5], recv_sems.at[5], device_id={"lon": 2 * t + c, "lat": y, "lev": x},
        ).start()
        return carry

    lax.fori_loop(1, 16, send_planes, 0)
    rm[pl.ds(pl.multiple_of(16 * slot, 16), 16), :] = mb[pl.ds(pl.multiple_of(16 * z, 16), 16), :]
    drain(rm.at[pl.ds(0, 240), :], recv_sems.at[5])

    for block in range(4):
        parts = []
        for i8 in (2 * block, 2 * block + 1):
            t00 = rm[pl.ds(i8, 8, stride=16), :]
            t01 = rm[pl.ds(8 + i8, 8, stride=16), :]
            t10 = rm[pl.ds(128 + i8, 8, stride=16), :]
            t11 = rm[pl.ds(128 + 8 + i8, 8, stride=16), :]
            parts.append(jnp.concatenate([
                jnp.where(half, t00, pltpu.roll(t10, 64, 1)),
                jnp.where(half, pltpu.roll(t00, 64, 1), t10),
                jnp.where(half, t01, pltpu.roll(t11, 64, 1)),
            ], axis=0))
        inputs = jnp.concatenate(parts, axis=1).astype(BF16)
        hidden = silu(mm(w_in[...], inputs)).astype(BF16)
        hidden = silu(mm(w_mid[0], hidden)).astype(BF16)
        hidden = silu(mm(w_mid[1], hidden)).astype(BF16)
        result = mm(w_out[...], hidden).astype(BF16).astype(F32)
        for n in range(2):
            for f in range(3):
                row = (f * 8 + 2 * block + n) * 8
                cr[row : row + 8, :] = result[8 * f : 8 * f + 8, 128 * n : 128 * n + 128]

    for l in range(LEVELS):
        t00 = rm[16 * l : 16 * l + 8, :]
        t01 = rm[16 * l + 8 : 16 * l + 16, :]
        t10 = rm[128 + 16 * l : 128 + 16 * l + 8, :]
        t11 = rm[128 + 16 * l + 8 : 128 + 16 * l + 16, :]
        s = [
            jnp.where(half, t00, pltpu.roll(t10, 64, 1)),
            jnp.where(half, pltpu.roll(t00, 64, 1), t10),
            jnp.where(half, t01, pltpu.roll(t11, 64, 1)),
        ]
        s = [s[f] + cr[pl.ds(64 * f + l, 8, stride=8), :] for f in range(3)]
        for bit in range(2):
            for core in range(2):
                n = 2 * bit + core
                value = pltpu.roll(s[0], (-32 * n) % 128, 1)
                for f in range(1, 3):
                    value = jnp.where(lane >= 32 * f, pltpu.roll(s[f], (32 * (f - n)) % 128, 1), value)
                row = (2 * (l // 2) + core) * 32 + (2 * (l % 2) + bit) * 8
                fb[row : row + 8, :] = value

    place = 2 * x + c

    def send_levels(j, carry):
        t = lax.rem(place + j, 8)
        pltpu.make_async_remote_copy(
            fb.at[pl.ds(pl.multiple_of(32 * t, 32), 32), :], ob.at[pl.ds(pl.multiple_of(32 * place, 32), 32), :],
            send_sems.at[6], recv_sems.at[6],
            device_id={"lon": 2 * z + lax.rem(t, 2), "lat": y, "lev": lax.div(t, 2)},
        ).start()
        return carry

    lax.fori_loop(1, 8, send_levels, 0)
    ob[pl.ds(pl.multiple_of(32 * place, 32), 32), :] = fb[pl.ds(pl.multiple_of(32 * place, 32), 32), :]
    drain(ob.at[pl.ds(0, 224), :], recv_sems.at[6])
    for b in range(2):
        rows = []
        for k in range(16):
            row = (2 * (k // 4) + k % 2) * 32 + (2 * b + (k // 2) % 2) * 8
            rows.append(ob[row : row + 8, :])
        stage[...] = jnp.concatenate(rows, axis=0).T
        for f in range(3):
            out_ref[f, b] = stage[32 * f : 32 * f + 30, :]

    @pl.when(own_first)
    def _():
        drain(at.at[pl.ds(0, 248), :], send_sems.at[0])

    @pl.when(jnp.logical_not(own_first))
    def _():
        drain(at, send_sems.at[0])

    for n in range(4):
        drain(vb.at[n, pl.ds(0, 2 * GROUP - 2), :], send_sems.at[1 + n])
    drain(mb.at[pl.ds(0, 240), :], send_sems.at[5])
    drain(fb.at[pl.ds(0, 224), :], send_sems.at[6])


def per_device(fields, spectral_coeffs, mlp_in, mlp_mid, mlp_out):
    zonal, fwd, inv, gather, scatter = (jnp.asarray(t) for t in host_tables())
    anywhere = pl.BlockSpec(memory_space=pl.ANY)
    vmem = lambda *shape: pltpu.VMEM(shape, F32)
    return pl.pallas_call(
        kernel,
        out_shape=jax.ShapeDtypeStruct(fields.shape, F32),
        in_specs=[pl.BlockSpec(memory_space=pltpu.SMEM)] + [anywhere] * 9,
        out_specs=pl.BlockSpec(memory_space=pltpu.VMEM),
        scratch_shapes=[
            pltpu.VMEM(fields.shape, F32),
            pltpu.VMEM(zonal.shape, BF16),
            pltpu.VMEM(fwd.shape[1:], BF16),
            pltpu.VMEM(inv.shape[1:], BF16),
            pltpu.VMEM(gather.shape, BF16),
            pltpu.VMEM(scatter.shape, BF16),
            pltpu.VMEM(mlp_in.shape, BF16),
            pltpu.VMEM(mlp_mid.shape, BF16),
            pltpu.VMEM(mlp_out.shape, BF16),
            vmem(128, 128),
            vmem(256, 128),
            vmem(256, 128),
            vmem(24, 1024),
            vmem(4, 128, 128),
            vmem(4, 128, 128),
            vmem(2, KMAX, 32),
            vmem(256, 128),
            vmem(256, 128),
            vmem(192, 128),
            vmem(256, 128),
            vmem(256, 128),
            pltpu.SemaphoreType.DMA((9,)),
            pltpu.SemaphoreType.DMA((7,)),
            pltpu.SemaphoreType.DMA((7,)),
        ],
        compiler_params=pltpu.CompilerParams(
            collective_id=0, has_side_effects=True, vmem_limit_bytes=56 * 1024 * 1024
        ),
        cost_estimate=pl.CostEstimate(flops=10**9, bytes_accessed=8 * 10**6, transcendentals=10**6),
    )(spectral_coeffs, fields, zonal, fwd, inv, gather, scatter, mlp_in, mlp_mid, mlp_out)


def solution(mesh):
    in_specs = (P(None, "lev", "lon", "lat"), P(None, "lev"), P(), P(), P())
    out_specs = P(None, "lev", "lon", "lat")
    return jax.shard_map(per_device, mesh=mesh, in_specs=in_specs, out_specs=out_specs, check_vma=False)
```

profile of v0, /device:TPU:1, one launch (start us, length us, event | category | flops | bytes accessed | tf_op | source)
XLA Modules:
  0.0 86.0 jit_solution(9631595483299700515)
XLA Ops:
  0.0 1.3 %copy.11.coef_ref = f32[3,2]{1,0:T(4,128)} copy(f32[3,2]{0,1:T(2,128)} %param.11) | data formatting | bytes 48 | tf_op args[1]
  1.3 1.5 %copy.12.fields_hbm = f32[3,2,30,128]{3,2,1,0:T(8,128)} copy(f32[3,2,30,128]{3,1,2,0:T(2,128)} %param.10) | data formatting | bytes 184320 | tf_op args[0]
  2.9 1.5 %copy.13.w_in_hbm = bf16[384,24]{1,0:T(8,128)(2,1)} copy(bf16[384,24]{0,1:T(8,128)(2,1)} %param.12) | data formatting | bytes 36864 | tf_op args[2]
  4.3 80.1 %shard_map.100 = f32[3,2,30,128]{3,2,1,0:T(8,128)} custom-call(f32[3,2]{1,0:T(4,128)} %copy.11.coef_ref, f32[3,2,30,128]{3,2,1,0:T(8,128)} %copy.12.fields_hbm, bf16[2,640,1024]{2,1,0:T(8,128)(2,1)} %constant.10.clone.zonal_hbm, bf16[2,2,320,512]{3,2,1,0:T(8,128)(2,1)} %constant.11.clone.fwd_hbm, bf16[2,2,512,320]{3,2,1,0:T(8,128)(2,1)} %constant.12.clone.inv_hbm, ...), custom_call_target="tpu_custom_call" | custom-call | flops 1000000000 | bytes 8000000 | tf_op jit(solution)/shard_map/pallas_call | solution.py:387
  84.4 1.6 %copy.14 = f32[3,2,30,128]{3,1,2,0:T(2,128)} copy(f32[3,2,30,128]{3,2,1,0:T(8,128)} %shard_map.100) | data formatting | bytes 184320 | tf_op jit(solution)/shard_map/pallas_call | solution.py:387
where the time goes:
time: 86.3 us; the launch traced here: 86 us
  Pallas kernels  80.1 us (93%)
  local copies, waits for them, and re-layouts  5.92 us (7%)
    pallas_call x1, Pallas kernels, per_device(): pl.pallas_call(kernel, out_shape=jax.ShapeDtypeStruct(fields.shape, F32),...  80.1 us
    unnamed x3, local copies, waits for them, and re-layouts  4.31 us

commit v1 on v0

--- a/solution.py
+++ b/solution.py
@@ -1,8 +1,7 @@
-import functools
+import math
 
 import jax
 import jax.numpy as jnp
-import numpy as np
 from jax import lax
 from jax.experimental import pallas as pl
 from jax.experimental.pallas import tpu as pltpu
@@ -20,37 +19,16 @@
 BF16 = jnp.bfloat16
 
 
-def split_host(table):
-    high = table.astype(np.float32).astype(BF16)
-    low = (table - high.astype(np.float64)).astype(np.float32).astype(BF16)
-    return np.stack([high, low])
-
-
-@functools.lru_cache(None)
-def host_tables():
-    q = np.repeat(np.arange(10), GROUP)
-    o = np.tile(np.arange(GROUP), 10)
-    wave = 2 * (5 * (o // 2) + q % 5) + o % 2
-    lane = np.arange(1024)
-    lon = 30 * (lane // 32) + lane % 32
-    phase = (wave[:, None] * lon[None, :]) % NLON * (2.0 * np.pi / NLON)
-    zonal = np.where(q[:, None] < 5, np.cos(phase), -np.sin(phase)) * (lane % 32 < 30)[None, :]
-    pos = np.arange(NLAT)
-    lat = 8 * (pos % 64) + pos // 64
-    deg = np.arange(KMAX)
-    odd = 2 * lat + 1
-    even = np.cos((deg[:, None] * odd[None, :]) % (4 * NLAT) * (np.pi / (2 * NLAT)))
-    sine = np.sin(((deg[:, None] + 1) * odd[None, :]) % (4 * NLAT) * (np.pi / (2 * NLAT)))
-    fwd = np.stack([split_host(even), split_host(sine)])
-    inv = np.stack([split_host(even.T), split_host(sine.T)])
-    perm = np.zeros((10, 24, 256), np.float32)
-    for f in range(3):
-        for i8 in range(8):
-            for c in range(10):
-                perm[c, f * 8 + i8, i8 * 32 + f * 10 + c] = 1.0
-    gather = np.concatenate([perm, perm], axis=1).reshape(480, 256).astype(BF16)
-    scatter = perm.reshape(240, 256).astype(BF16)
-    return split_host(zonal), fwd, inv, gather, scatter
+SINE = [(-1.0) ** n * math.pi ** (2 * n + 1) / math.factorial(2 * n + 1) for n in range(7)]
+
+
+def cosine(half_turns):
+    t = jnp.abs(half_turns - 1.0) - 0.5
+    square = t * t
+    value = jnp.full(t.shape, SINE[-1], F32)
+    for term in SINE[-2::-1]:
+        value = value * square + term
+    return value * t
 
 
 def split(value):
@@ -71,9 +49,9 @@
 
 
 def kernel(
-    coef_ref, fields_hbm, zonal_hbm, fwd_hbm, inv_hbm, gather_hbm, scatter_hbm, w_in_hbm, w_mid_hbm, w_out_hbm,
+    coef_ref, fields_hbm, w_in_hbm, w_mid_hbm, w_out_hbm,
     out_ref,
-    fields, zonal, fwd, inv, gather, scatter, w_in, w_mid, w_out,
+    fields, zonal, fwd, inv, gather, scatter, w_turned, w_in, w_mid, w_out,
     stage, at, ra, state, vb, ub, mult, mb, rm, cr, fb, ob,
     load_sems, send_sems, recv_sems,
 ):
@@ -94,14 +72,9 @@
         loads.append(copy)
 
     load(0, fields_hbm, fields)
-    load(1, zonal_hbm, zonal)
-    load(2, fwd_hbm.at[c], fwd)
-    load(3, inv_hbm.at[c], inv)
-    load(4, gather_hbm, gather)
-    load(5, scatter_hbm, scatter)
-    load(6, w_in_hbm, w_in)
-    load(7, w_mid_hbm, w_mid)
-    load(8, w_out_hbm, w_out)
+    load(1, w_in_hbm, w_turned)
+    load(2, w_mid_hbm, w_mid)
+    load(3, w_out_hbm, w_out)
 
     def group_device(g):
         return {"lon": 4 * p + lax.rem(g, 4), "lat": lax.div(g, 16), "lev": lax.div(lax.rem(g, 16), 4)}
@@ -138,12 +111,64 @@
     loads[0].wait()
     for b in range(2):
         for f in range(3):
-            stage[32 * f : 32 * f + 30, :] = fields[f, b]
+            stage[32 * f : 32 * f + 30, :] = fields[f, :, b, :]
             stage[32 * f + 30 : 32 * f + 32, :] = jnp.zeros((2, 128), F32)
         for n in range(3):
-            stage[96 + n : 97 + n, :] = jnp.full((1, 128), coef_ref[n, b], F32)
+            stage[96 + n : 97 + n, :] = jnp.full((1, 128), coef_ref[b, n], F32)
         stage[99:128, :] = jnp.zeros((29, 128), F32)
         at[128 * b : 128 * b + 128, :] = stage[...].T
+
+    def zonal_block(n, carry):
+        turn, v = lax.div(n, 8), lax.rem(n, 8)
+        owner = lax.broadcasted_iota(jnp.int32, (GROUP, 128), 0)
+        place = lax.broadcasted_iota(jnp.int32, (GROUP, 128), 1)
+        wave = 2 * (5 * lax.shift_right_logical(owner, 1) + turn) + (owner & 1)
+        r = place & 31
+        lon = 30 * (4 * v + lax.shift_right_logical(place, 5)) + r
+        product = (wave * lon).astype(F32)
+        turns = product - NLON * jnp.floor(product * (1.0 / NLON))
+        quarter = jnp.where(turns >= 0.75 * NLON, turns - 0.75 * NLON, turns + 0.25 * NLON)
+        for row, steps in ((turn, turns), (5 + turn, quarter)):
+            value = jnp.where(r < 30, cosine(steps * (2.0 / NLON)), 0.0)
+            high, low = split(value)
+            rows = pl.ds(pl.multiple_of(GROUP * row, GROUP), GROUP)
+            lanes = pl.ds(pl.multiple_of(128 * v, 128), 128)
+            zonal[0, rows, lanes] = high
+            zonal[1, rows, lanes] = low
+        return carry
+
+    def latitude(deg, place):
+        odd = 2 * (8 * (place & 63) + lax.shift_right_logical(place, 6)) + 1
+        steps = ((deg + c) * odd - 512 * c) & (4 * NLAT - 1)
+        return split(cosine(steps.astype(F32) * (1.0 / (2 * NLAT))))
+
+    def fwd_block(n, carry):
+        rows = pl.ds(pl.multiple_of(32 * n, 32), 32)
+        deg = 32 * n + lax.broadcasted_iota(jnp.int32, (32, NLAT), 0)
+        high, low = latitude(deg, lax.broadcasted_iota(jnp.int32, (32, NLAT), 1))
+        fwd[0, rows, :] = high
+        fwd[1, rows, :] = low
+        return carry
+
+    def inv_block(n, carry):
+        rows = pl.ds(pl.multiple_of(32 * n, 32), 32)
+        place = 32 * n + lax.broadcasted_iota(jnp.int32, (32, KMAX), 0)
+        high, low = latitude(lax.broadcasted_iota(jnp.int32, (32, KMAX), 1), place)
+        inv[0, rows, :] = high
+        inv[1, rows, :] = low
+        return carry
+
+    def lane_tables():
+        row = lax.broadcasted_iota(jnp.int32, (24, 256), 0)
+        place = lax.broadcasted_iota(jnp.int32, (24, 256), 1)
+        base = (row & 7) * 32 + lax.shift_right_logical(row, 3) * 10
+        for q in range(10):
+            hit = jnp.where(place == base + q, 1.0, 0.0)
+            gather[48 * q : 48 * q + 48, :] = jnp.concatenate([hit, hit], axis=0).astype(BF16)
+            scatter[24 * q : 24 * q + 24, :] = hit
+
+    lax.fori_loop(0, 40, zonal_block, 0)
+    lane_tables()
 
     pl.semaphore_wait(barrier, 31 + jnp.where(own_first, 0, 1) + (GROUP - 1) + 15)
 
@@ -168,8 +193,11 @@
     def drain(ref, sem):
         pltpu.make_async_copy(ref, ref, sem).wait()
 
-    for n in range(1, 9):
+    lax.fori_loop(0, 10, fwd_block, 0)
+    lax.fori_loop(0, 16, inv_block, 0)
+    for n in range(1, 4):
         loads[n].wait()
+    w_in[...] = w_turned[...].astype(F32).T.astype(BF16)
 
     @pl.when(own_first)
     def _():
@@ -267,8 +295,8 @@
         value = received(c_in)
 
         high, low = split(value)
-        y_high = mm_nt(scatter[...], high)
-        y_low = mm_nt(scatter[...], low)
+        y_high = mm_nt(scatter[...].astype(BF16), high)
+        y_low = mm_nt(scatter[...].astype(BF16), low)
         y_high = jnp.concatenate([y_high[24 * q : 24 * q + 24] for q in range(10)], axis=1)
         y_low = jnp.concatenate([y_low[24 * q : 24 * q + 24] for q in range(10)], axis=1)
         both = jnp.concatenate([y_high, y_low], axis=0).astype(BF16)
@@ -364,7 +392,7 @@
             rows.append(ob[row : row + 8, :])
         stage[...] = jnp.concatenate(rows, axis=0).T
         for f in range(3):
-            out_ref[f, b] = stage[32 * f : 32 * f + 30, :]
+            out_ref[f, :, b, :] = stage[32 * f : 32 * f + 30, :]
 
     @pl.when(own_first)
     def _():
@@ -381,24 +409,26 @@
 
 
 def per_device(fields, spectral_coeffs, mlp_in, mlp_mid, mlp_out):
-    zonal, fwd, inv, gather, scatter = (jnp.asarray(t) for t in host_tables())
     anywhere = pl.BlockSpec(memory_space=pl.ANY)
     vmem = lambda *shape: pltpu.VMEM(shape, F32)
-    return pl.pallas_call(
+    half = lambda *shape: pltpu.VMEM(shape, BF16)
+    fields = fields.transpose(0, 2, 1, 3)
+    updated = pl.pallas_call(
         kernel,
         out_shape=jax.ShapeDtypeStruct(fields.shape, F32),
-        in_specs=[pl.BlockSpec(memory_space=pltpu.SMEM)] + [anywhere] * 9,
+        in_specs=[pl.BlockSpec(memory_space=pltpu.SMEM)] + [anywhere] * 4,
         out_specs=pl.BlockSpec(memory_space=pltpu.VMEM),
         scratch_shapes=[
-            pltpu.VMEM(fields.shape, F32),
-            pltpu.VMEM(zonal.shape, BF16),
-            pltpu.VMEM(fwd.shape[1:], BF16),
-            pltpu.VMEM(inv.shape[1:], BF16),
-            pltpu.VMEM(gather.shape, BF16),
-            pltpu.VMEM(scatter.shape, BF16),
-            pltpu.VMEM(mlp_in.shape, BF16),
-            pltpu.VMEM(mlp_mid.shape, BF16),
-            pltpu.VMEM(mlp_out.shape, BF16),
+            vmem(*fields.shape),
+            half(2, 2 * WAVES, 1024),
+            half(2, KMAX, NLAT),
+            half(2, NLAT, KMAX),
+            half(480, 256),
+            vmem(240, 256),
+            half(3 * LEVELS, UNITS),
+            half(UNITS, 3 * LEVELS),
+            half(2, UNITS, UNITS),
+            half(3 * LEVELS, UNITS),
             vmem(128, 128),
             vmem(256, 128),
             vmem(256, 128),
@@ -411,7 +441,7 @@
             vmem(192, 128),
             vmem(256, 128),
             vmem(256, 128),
-            pltpu.SemaphoreType.DMA((9,)),
+            pltpu.SemaphoreType.DMA((4,)),
             pltpu.SemaphoreType.DMA((7,)),
             pltpu.SemaphoreType.DMA((7,)),
         ],
@@ -419,7 +449,8 @@
             collective_id=0, has_side_effects=True, vmem_limit_bytes=56 * 1024 * 1024
         ),
         cost_estimate=pl.CostEstimate(flops=10**9, bytes_accessed=8 * 10**6, transcendentals=10**6),
-    )(spectral_coeffs, fields, zonal, fwd, inv, gather, scatter, mlp_in, mlp_mid, mlp_out)
+    )(spectral_coeffs.T, fields, mlp_in.T, mlp_mid, mlp_out)
+    return updated.transpose(0, 2, 1, 3)
 
 
 def solution(mesh):

time: 86.3 us -> 81.7 us (0.947)
  local copies, waits for them, and re-layouts: 5.92 us -> 1.54 us
    unnamed x3 -> x1, local copies, waits for them, and re-layouts: 4.31 us -> 1.54 us
    pallas_call x1 -> x0, local copies, waits for them, and re-layouts: 1.6 us -> none  [per_device(): pl.pallas_call(kernel, out_shape=jax.ShapeDtypeStruct(fields.shape, F32),...]
where the time goes in v1:
time: 81.7 us; the launch traced here: 81.5 us
  Pallas kernels  79.9 us (98%)
  local copies, waits for them, and re-layouts  1.54 us (2%)
    pallas_call x1, Pallas kernels, per_device(): pl.pallas_call(kernel, out_shape=jax.ShapeDtypeStruct(fields.shape, F32),...  79.9 us

profile of v1, /device:TPU:1, one launch (start us, length us, event | category | flops | bytes accessed | tf_op | source)
XLA Modules:
  0.0 81.5 jit_solution(16734940128452338274)
XLA Ops:
  0.0 79.9 %shard_map.55 = f32[3,30,2,128]{3,2,1,0:T(2,128)} custom-call(f32[2,3]{1,0:T(2,128)} %bitcast.7, f32[3,30,2,128]{3,2,1,0:T(2,128)} %bitcast.5, bf16[24,384]{1,0:T(8,128)(2,1)} %bitcast.6, bf16[2,384,384]{2,1,0:T(8,128)(2,1)} %w_mid_hbm.1, bf16[24,384]{1,0:T(8,128)(2,1)} %w_out_hbm.1), custom_call_target="tpu_custom_call" | custom-call | flops 1000000000 | bytes 8000000 | tf_op jit(solution)/shard_map/pallas_call | solution.py:416
  80.0 1.5 %copy.7 = f32[3,2,30,128]{3,1,2,0:T(2,128)} copy(f32[3,2,30,128]{3,1,2,0:T(2,128)} %bitcast.4) | data formatting | bytes 184320
